TPU v7x, 32 devices: a whole 2x2x4 slice. The times are simulated.
32 devices in a mesh: dp: 4 (over x, y), tp: 8 (over z, core).
Axes of the slice: x: 2, y: 2, z: 4, core: 2. Of those that a mesh axis runs over, the one named last changes fastest.
Arguments:
- x: bfloat16 [8192, 2048], P('dp'), parts along dimension 0
- dy: bfloat16 [8192, 2048], P('dp'), parts along dimension 0
- gate: bfloat16 [8192, 8192], P('dp', 'tp'), parts along dimension 0
- up: bfloat16 [8192, 8192], P('dp', 'tp'), parts along dimension 0
- w_gate: bfloat16 [2048, 8192], P(None, 'tp')
- w_up: bfloat16 [2048, 8192], P(None, 'tp')
- w_down: bfloat16 [8192, 2048], P('tp')
Outputs:
- output 1: bfloat16 [8192, 2048], P('dp'), parts along dimension 0
- output 2: bfloat16 [8192, 8192], P('dp', 'tp'), parts along dimension 0
- output 3: bfloat16 [8192, 8192], P('dp', 'tp'), parts along dimension 0
- output 4: bfloat16 [32768, 2048], P(('dp', 'tp')), parts along dimension 0
There are 4 independent parts. A program takes and returns all parts, laid end to end along the dimension named above; an argument that names none is the same for every part.
All inputs are finite; a program needn't handle non-finite values.
Results may differ from a plain program's by a relative error of at most 0.012.
Values are sent between devices in bfloat16 or wider.
A program may use at most 2 GiB of HBM per device.

v0:
```python
import jax
import jax.numpy as jnp
from jax import lax
from jax.sharding import PartitionSpec as P


def act(gate, up):
    return jax.nn.silu(gate) * up


def solution(mesh):
    def step(x, dy, gate, up, w_gate, w_up, w_down):
        hidden, back = jax.vjp(act, gate.astype(jnp.float32), up.astype(jnp.float32))
        d_hidden = jnp.dot(dy, w_down.T, preferred_element_type=jnp.float32)
        d_gate, d_up = (g.astype(jnp.bfloat16) for g in back(d_hidden))
        term = jnp.dot(d_gate, w_gate.T, preferred_element_type=jnp.float32) + jnp.dot(d_up, w_up.T, preferred_element_type=jnp.float32)
        dx = lax.psum(term.astype(jnp.bfloat16), "tp")
        dw_gate = jnp.dot(x.T, d_gate, preferred_element_type=jnp.float32)
        dw_up = jnp.dot(x.T, d_up, preferred_element_type=jnp.float32)
        dw_down = jnp.dot(hidden.astype(jnp.bfloat16).T, dy, preferred_element_type=jnp.float32)
        return dx, *(g.astype(jnp.bfloat16) for g in (dw_gate, dw_up, dw_down))

    tokens, columns, rows = P("dp", None), P(None, "tp"), P("tp", None)
    return jax.shard_map(
        step,
        mesh=mesh,
        in_specs=(tokens, tokens, P("dp", "tp"), P("dp", "tp"), columns, columns, rows),
        out_specs=(tokens, P("dp", "tp"), P("dp", "tp"), P(("dp", "tp"), None)),
        check_vma=False,
    )
```

profile of v0, /device:TPU:0, one launch (start us, length us, event | category | flops | bytes accessed | tf_op | source)
XLA Modules:
  0.0 253.2 jit_solution(1383775611010362306)
XLA Ops:
  7.2 0.0 all-reduce.2.cloned.1.call-start
  7.2 0.0 copy-start
  7.2 20.2 %fusion.6 = (bf16[2048,1024]{1,0:T(8,128)(2,1)S(1)}, f32[2048,1024]{1,0:T(8,128)}) fusion(bf16[2048,1024]{1,0:T(8,128)(2,1)} %param.9, bf16[2048,1024]{1,0:T(8,128)(2,1)} %param.10, bf16[2048,2048]{1,0:T(8,128)(2,1)} %param.8, bf16[1024,2048]{1,0:T(8,128)(2,1)} %param.13), kind=kOutput, calls=%fused_computation.13 | convolution fusion | flops 8617197568 | bytes 33554432 | tf_op jit(solution)/shard_map/dot_general | solution.py:14
  27.4 0.0 copy-start.1
  27.4 0.0 copy-done
  27.4 11.7 %fusion.13 = f32[2048,2048]{1,0:T(8,128)} fusion(bf16[2048,1024]{1,0:T(8,128)(2,1)S(1)} %get-tuple-element.8, bf16[2048,1024]{1,0:T(8,128)(2,1)S(1)} %copy-done), kind=kOutput, calls=%fused_computation.20 | convolution fusion | flops 8589934592 | bytes 25165824 | tf_op jit(solution)/shard_map/dot_general | solution.py:16
  39.2 0.0 copy-done.1
  39.2 20.5 %add_convert_fusion = bf16[2048,2048]{1,0:T(8,128)(2,1)} fusion(f32[2048,2048]{1,0:T(8,128)} %fusion.13, bf16[2048,1024]{1,0:T(8,128)(2,1)} %param.12, f32[2048,1024]{1,0:T(8,128)} %get-tuple-element.9, bf16[2048,1024]{1,0:T(8,128)(2,1)} %param.9), kind=kOutput, calls=%fused_computation | convolution fusion | flops 8613003264 | bytes 41943040 | tf_op jit(solution)/shard_map/dot_general | solution.py:16
  59.7 0.0 all-reduce.2.cloned.1.call-update
  59.7 14.0 %convert_bitcast_fusion.1 = bf16[2048,1024]{0,1:T(8,128)(2,1)} fusion(bf16[2048,1024]{1,0:T(8,128)(2,1)} %copy-done.1, bf16[2048,2048]{1,0:T(8,128)(2,1)} %param.7), kind=kOutput, calls=%fused_computation.17 | convolution fusion | flops 8592031744 | bytes 16777216 | tf_op jit(solution)/shard_map/dot_general | solution.py:18
  73.7 6.4 %copy.11 = bf16[2048,1024]{1,0:T(8,128)(2,1)} copy(bf16[2048,1024]{0,1:T(8,128)(2,1)} %convert_bitcast_fusion.1) | data formatting | bytes 8388608
  80.1 16.4 %convert_bitcast_fusion = bf16[2048,1024]{0,1:T(8,128)(2,1)} fusion(bf16[2048,2048]{1,0:T(8,128)(2,1)} %param.7, f32[2048,1024]{1,0:T(8,128)} %get-tuple-element.9, bf16[2048,1024]{1,0:T(8,128)(2,1)} %param.9), kind=kOutput, calls=%fused_computation.16 | convolution fusion | flops 8606711808 | bytes 25165824 | tf_op jit(solution)/shard_map/dot_general | solution.py:19
  96.5 6.4 %copy.12 = bf16[2048,1024]{1,0:T(8,128)(2,1)} copy(bf16[2048,1024]{0,1:T(8,128)(2,1)} %convert_bitcast_fusion) | data formatting | bytes 8388608
  102.9 16.2 %fusion.9 = bf16[1024,2048]{1,0:T(8,128)(2,1)} fusion(bf16[2048,2048]{1,0:T(8,128)(2,1)} %param.8, bf16[2048,1024]{1,0:T(8,128)(2,1)} %param.10, bf16[2048,1024]{1,0:T(8,128)(2,1)} %param.9), kind=kOutput, calls=%fused_computation.18 | convolution fusion | flops 8608808960 | bytes 20971520 | tf_op jit(solution)/shard_map/dot_general | solution.py:20
  119.2 118.8 %all-reduce.2.cloned.1.call-done = bf16[2048,2048]{1,0:T(8,128)(2,1)} async-done(((bf16[2048,2048]{1,0:T(8,128)(2,1)}), bf16[2048,2048]{1,0:T(8,128)(2,1)}) %all-reduce.2.cloned.1.call-update) | async-done | bytes 8388624 | tf_op jit(solution)/shard_map/psum | solution.py:17
  238.0 8.4 %copy.14 = bf16[2048,2048]{1,0:T(8,128)(2,1)} copy(bf16[2048,2048]{1,0:T(8,128)(2,1)} %all-reduce.2.cloned.1.call-done) | data formatting | bytes 16777216
Async XLA Ops:
  7.2 230.8 %all-reduce.2.cloned.1.call-start = ((), (), s32[]{:S(2)}) async-start(), calls=%async_computation | async-start | bytes 16777216 | tf_op jit(solution)/shard_map/psum | solution.py:17
  7.2 20.2 %copy-start = (bf16[2048,1024]{1,0:T(8,128)(2,1)S(1)}, bf16[2048,1024]{1,0:T(8,128)(2,1)}, u32[]{:S(2)}) copy-start(bf16[2048,1024]{1,0:T(8,128)(2,1)} %param.11) | copy-start | bytes 12582916
  27.4 11.8 %copy-start.1 = (bf16[2048,1024]{1,0:T(8,128)(2,1)}, bf16[2048,1024]{1,0:T(8,128)(2,1)S(1)}, u32[]{:S(2)}) copy-start(bf16[2048,1024]{1,0:T(8,128)(2,1)S(1)} %get-tuple-element.8) | copy-start | bytes 12582916
Sparse Core Ops, SparseCore 0:
  59.8 178.0 all-reduce.1
where the time goes:
time: 254 us; the launch traced here: 253 us
  waiting for transfers between devices  119 us (47%)
  matrix products  99.1 us (39%)
  local copies, waits for them, and re-layouts  21.2 us (8%)
  between operations  14 us (6%)
    psum x1, waiting for transfers between devices, step(): dx = lax.psum(term.astype(jnp.bfloat16), 'tp')  119 us
    unnamed x7, local copies, waits for them, and re-layouts  21.2 us
    dot_general x1, matrix products, step(): jnp.dot(d_up, w_up.T, preferred_element_type=jnp.float32)  20.5 us
    dot_general x1, matrix products, step(): d_hidden = jnp.dot(dy, w_down.T, preferred_element_type=jnp.float32)  20.2 us
    dot_general x1, matrix products, step(): dw_up = jnp.dot(x.T, d_up, preferred_element_type=jnp.float32)  16.4 us
    dot_general x1, matrix products, step(): jnp.dot(hidden.astype(jnp.bfloat16).T, dy, preferred_element_type=jnp.flo...  16.2 us
    dot_general x1, matrix products, step(): dw_gate = jnp.dot(x.T, d_gate, preferred_element_type=jnp.float32)  14 us
    dot_general x1, matrix products, step(): jnp.dot(d_gate, w_gate.T, preferred_element_type=jnp.float32)  11.7 us
  transfers between devices with their start and end apart: 1, of which 1 were waited for; matrix products, arithmetic and copies ran while one was open for 23% of the time, Pallas kernels for 0%

commit v1 on v0

v1 whole, which is shorter than its diff:
```python
import functools

import jax
import jax.numpy as jnp
from jax import lax
from jax.experimental import pallas as pl
from jax.experimental.pallas import tpu as pltpu
from jax.sharding import PartitionSpec as P

BF16, F32 = jnp.bfloat16, jnp.float32
MESH = pl.DeviceIdType.MESH
HALF = 1024
UNIT = 256
CHUNK = 128
NT = (((1,), (1,)), ((), ()))
NN = (((1,), (0,)), ((), ()))


def dot(a, b, dims):
    return lax.dot_general(a, b, dims, preferred_element_type=F32)


def kernel(
    x_ref, dy_ref, gate_ref, up_ref, wg_ref, wu_ref, wd_ref,
    dx_ref, dwg_ref, dwu_ref, dwd_ref,
    wd, w, dy, dg, du, hid, gu, own, stage, pt, rs, qb, ob,
    w_sem, dy_sem, gu_sem, x_sem, ob_sem, dx_sem,
    pt_send, pt_recv, rs_send, rs_recv, q_send, q_recv, dd_send, dd_recv,
):
    rows = dy_ref.shape[0]
    units, chunks = rows // UNIT, rows // CHUNK
    per = UNIT // CHUNK
    me = lax.axis_index("tp")
    z, c = me // 2, me % 2
    m = jnp.where(c == 1, z, 3 - z)
    first, last = m == 0, m == 3
    partner = z * 2 + 1 - c
    following = jnp.clip(z + 2 * c - 1, 0, 3) * 2 + c
    previous = jnp.clip(z - 2 * c + 1, 0, 3) * 2 + c
    mine = pl.multiple_of(c * HALF, HALF)
    other = pl.multiple_of((1 - c) * HALF, HALF)

    def span(i, n):
        return pl.ds(pl.multiple_of(i * n, n), n)

    def load_w(i):
        src, dst = ((wd_ref, wd), (wg_ref, w.at[0]), (wu_ref, w.at[1]))[i]
        return pltpu.make_async_copy(src, dst, w_sem.at[i])

    def load_dy(i):
        return pltpu.make_async_copy(dy_ref.at[span(i, UNIT)], dy.at[span(i, UNIT)], dy_sem.at[i])

    def load_gu(i, j):
        src = (gate_ref, up_ref)[j]
        slot = lax.rem(i, 2)
        return pltpu.make_async_copy(src.at[span(i, UNIT)], gu.at[slot, j], gu_sem.at[slot, j])

    def load_x(j):
        return pltpu.make_async_copy(x_ref.at[:, pl.ds(j * HALF, HALF)], w.at[j], x_sem.at[j])

    load_w(0).start()
    for i in range(2):
        load_dy(i).start()
        load_gu(i, 0).start()
        load_gu(i, 1).start()
        if i == 0:
            load_w(1).start()
            load_w(2).start()
    for i in range(2, units):
        load_dy(i).start()

    barrier = pltpu.get_barrier_semaphore()
    pl.semaphore_signal(barrier, inc=1, device_id={"tp": partner}, device_id_type=MESH)

    @pl.when(m < 3)
    def _():
        pl.semaphore_signal(barrier, inc=1, device_id={"tp": following}, device_id_type=MESH)

    @pl.when(m > 0)
    def _():
        pl.semaphore_signal(barrier, inc=1, device_id={"tp": previous}, device_id_type=MESH)

    pl.semaphore_wait(barrier, jnp.where(first | last, 2, 3))

    def remote(src, dst, send, recv, device):
        return pltpu.make_async_remote_copy(
            src_ref=src, dst_ref=dst, send_sem=send, recv_sem=recv,
            device_id={"tp": device}, device_id_type=MESH)

    def to_partner(k):
        r = span(k, CHUNK)
        return remote(stage.at[r], pt.at[r], pt_send.at[k], pt_recv.at[k], partner)

    def pass_sum(k):
        r = span(k, CHUNK)
        return remote(pt.at[r], rs.at[r], rs_send.at[k], rs_recv.at[k], following)

    def turn(k):
        r = span(k, CHUNK)
        return remote(pt.at[r], qb.at[r], rs_send.at[k], q_recv.at[k], partner)

    def pass_result(k):
        r = span(k, CHUNK)
        return remote(qb.at[r], qb.at[r], q_send.at[k], q_recv.at[k], following)

    def share_result(k):
        r = span(k, CHUNK)
        return remote(qb.at[r], dx_ref.at[r, pl.ds(other, HALF)], dd_send.at[k], dd_recv.at[k], partner)

    def keep_result(k):
        r = span(k, CHUNK)
        return pltpu.make_async_copy(qb.at[r], dx_ref.at[r, pl.ds(other, HALF)], dx_sem.at[0, k])

    def keep_sum(k):
        r = span(k, CHUNK)
        return pltpu.make_async_copy(pt.at[r], dx_ref.at[r, pl.ds(mine, HALF)], dx_sem.at[1, k])

    def sum_step(k, _):
        r = span(k, CHUNK)
        to_partner(k).wait_recv()

        @pl.when(first)
        def _():
            pt[r] = (own[r] + pt[r].astype(F32)).astype(BF16)

        @pl.when(m > 0)
        def _():
            pass_sum(k).wait_recv()
            pt[r] = (own[r] + pt[r].astype(F32) + rs[r].astype(F32)).astype(BF16)

        @pl.when(m < 3)
        def _():
            pass_sum(k).start()

        @pl.when(last)
        def _():
            turn(k).start()
            keep_sum(k).start()

        return 0

    def result_step(k, _):
        pass_result(k).wait_recv()

        @pl.when(m < 3)
        def _():
            pass_result(k).start()

        @pl.when(m > 0)
        def _():
            share_result(k).start()

        keep_result(k).start()
        return 0

    def paced(s):
        return jnp.maximum((s - 2 - 4 * m) * 4 + 9, 0) // 9

    def early(s):
        cap = per * ((s + 1) // 3)
        lead = jnp.where(s < 3, cap, per * (s // 3))
        return jnp.where(first, lead, jnp.minimum(paced(s), cap))

    def late(s):
        return jnp.clip(jnp.where(first, jnp.maximum(paced(s), chunks), paced(s)), 0, 2 * chunks)

    def serve(lo, hi):
        lax.fori_loop(jnp.minimum(lo, chunks), jnp.minimum(hi, chunks), sum_step, 0)
        lax.fori_loop(jnp.maximum(lo, chunks) - chunks, jnp.maximum(hi, chunks) - chunks, result_step, 0)

    def serve_sums(s):
        lax.fori_loop(early(s - 1), early(s), sum_step, 0)

    load_w(0).wait()

    def unit(u, _):
        r = span(u, UNIT)
        slot = lax.rem(u, 2)
        load_dy(u).wait()
        load_gu(u, 0).wait()
        load_gu(u, 1).wait()
        n = 512
        for b in range(0, HALF, n):
            f = slice(b, b + n)
            dh = dot(dy[r, :], wd[f, :], NT)
            gate = gu[slot, 0, :, f].astype(F32)
            up = gu[slot, 1, :, f].astype(F32)
            sig = jax.nn.sigmoid(gate)
            silu = gate * sig
            hid[r, f] = (silu * up).astype(BF16)
            du[r, f] = (dh * silu).astype(BF16)
            dg[r, f] = ((dh * up) * (sig * (1.0 + gate * (1.0 - sig)))).astype(BF16)

        @pl.when(u + 2 < units)
        def _():
            load_gu(u + 2, 0).start()
            load_gu(u + 2, 1).start()

        serve_sums(3 * u)

        @pl.when(u == 0)
        def _():
            load_w(1).wait()
            load_w(2).wait()

        stage[r] = (dot(dg[r], w[0, pl.ds(other, HALF), :], NT) + dot(du[r], w[1, pl.ds(other, HALF), :], NT)).astype(BF16)
        for j in range(per):
            to_partner(u * per + j).start()
        serve_sums(3 * u + 1)
        own[r] = dot(dg[r], w[0, pl.ds(mine, HALF), :], NT) + dot(du[r], w[1, pl.ds(mine, HALF), :], NT)
        serve_sums(3 * u + 2)
        return 0

    lax.fori_loop(0, units, unit, 0)
    for j in range(2):
        load_x(j).start()

    slots = 3 * units

    def put(i, dst):
        s = lax.rem(i, 2)
        return pltpu.make_async_copy(ob.at[s], dst, ob_sem.at[s])

    def down_dst(i):
        return dwd_ref.at[span(i // 2, UNIT), span(lax.rem(i, 2), HALF)]

    n_down = 2 * HALF // UNIT

    def down(i, _):
        @pl.when(i >= 2)
        def _():
            put(i, down_dst(0)).wait()

        left = hid[:, span(i // 2, UNIT)].T
        ob[lax.rem(i, 2)] = dot(left, dy[:, span(lax.rem(i, 2), HALF)], NN).astype(BF16)
        put(i, down_dst(i)).start()
        s = slots + i
        serve(jnp.where(i == 0, early(s - 1), late(s - 1)), late(s))
        return 0

    lax.fori_loop(0, n_down, down, 0)
    for j in range(2):
        load_x(j).wait()
    blocks = HALF // UNIT

    def side(j, right, dst):
        def body(i, _):
            put(i, dst.at[span(0, UNIT)]).wait()
            left = w[i // blocks, :, span(lax.rem(i, blocks), UNIT)].T
            ob[lax.rem(i, 2)] = dot(left, right[...], NN).astype(BF16)
            put(i, dst.at[span(i, UNIT)]).start()
            s = slots + n_down + j * 2 * blocks + i
            serve(late(s - 1), late(s))
            return 0

        lax.fori_loop(0, 2 * blocks, body, 0)

    side(0, dg, dwg_ref)
    side(1, du, dwu_ref)
    serve(late(slots + n_down + 4 * blocks - 1), 2 * chunks)

    for i in range(2):
        put(i, dwu_ref.at[span(0, UNIT)]).wait()

    def drain(k, _):
        to_partner(k).wait_send()
        keep_result(k).wait()

        @pl.when(m < 3)
        def _():
            pass_sum(k).wait_send()
            pass_result(k).wait_send()
            share_result(k).wait_recv()

        @pl.when(last)
        def _():
            turn(k).wait_send()
            keep_sum(k).wait()

        @pl.when(m > 0)
        def _():
            share_result(k).wait_send()

        return 0

    lax.fori_loop(0, chunks, drain, 0)


def backward(x, dy, gate, up, w_gate, w_up, w_down):
    rows, d = x.shape
    ff = w_down.shape[0]
    units, chunks = rows // UNIT, rows // CHUNK
    any_ = pl.BlockSpec(memory_space=pltpu.HBM)
    dma = pltpu.SemaphoreType.DMA
    half = pltpu.VMEM((rows, HALF), BF16)
    return pl.pallas_call(
        kernel,
        out_shape=[
            jax.ShapeDtypeStruct((rows, d), BF16),
            jax.ShapeDtypeStruct((d, ff), BF16),
            jax.ShapeDtypeStruct((d, ff), BF16),
            jax.ShapeDtypeStruct((ff, d), BF16),
        ],
        in_specs=[any_] * 7,
        out_specs=[any_] * 4,
        scratch_shapes=[
            pltpu.VMEM((ff, d), BF16),
            pltpu.VMEM((2, d, ff), BF16),
            pltpu.VMEM((rows, d), BF16),
            half, half, half,
            pltpu.VMEM((2, 2, UNIT, ff), BF16),
            pltpu.VMEM((rows, HALF), F32),
            half, half, half, half,
            pltpu.VMEM((2, UNIT, HALF), BF16),
            dma((3,)), dma((units,)), dma((2, 2)), dma((2,)), dma((2,)), dma((2, chunks)),
        ] + [dma((chunks,))] * 8,
        compiler_params=pltpu.CompilerParams(
            collective_id=0, has_side_effects=True, vmem_limit_bytes=67043328),
        name="mlp_backward",
    )(x, dy, gate, up, w_gate, w_up, w_down)


def solution(mesh):
    tokens, columns, rows = P("dp", None), P(None, "tp"), P("tp", None)
    return jax.shard_map(
        backward,
        mesh=mesh,
        in_specs=(tokens, tokens, P("dp", "tp"), P("dp", "tp"), columns, columns, rows),
        out_specs=(tokens, P("dp", "tp"), P("dp", "tp"), P(("dp", "tp"), None)),
        check_vma=False,
    )
```

time: 254 us -> 144 us (0.57)
  Pallas kernels: 0 us -> 125 us
  waiting for transfers between devices: 119 us -> 0 us
  matrix products: 99.1 us -> 0 us
  between operations: 14 us -> 0.65 us
  local copies, waits for them, and re-layouts: 21.2 us -> 18 us
    pallas_call x0 -> x1, Pallas kernels: none -> 125 us  [backward(): pl.pallas_call(kernel, out_shape=[jax.ShapeDtypeStruct((rows, d), BF16),...]
    psum x1 -> x0, waiting for transfers between devices: 119 us -> none  [step(): dx = lax.psum(term.astype(jnp.bfloat16), 'tp')]
    dot_general x6 -> x0, matrix products: 99.1 us -> none  [the longest x1 20.5 us: step(): jnp.dot(d_up, w_up.T, preferred_element_type=jnp.float32)]
    unnamed x7 -> x10, local copies, waits for them, and re-layouts: 21.2 us -> 18 us
  transfers between devices with their start and end apart: 1 -> 0, of which waited for: 1 -> 0; matrix products, arithmetic and copies ran while one was open for 23% -> 0% of each run, Pallas kernels for 0% -> 0%
where the time goes in v1:
time: 144 us
  Pallas kernels  125 us (87%)
  local copies, waits for them, and re-layouts  18 us (12%)
    pallas_call x1, Pallas kernels, backward(): pl.pallas_call(kernel, out_shape=[jax.ShapeDtypeStruct((rows, d), BF16),...  125 us
    unnamed x10, local copies, waits for them, and re-layouts  18 us

profile of v1, /device:TPU:0, one launch (start us, length us, event | category | flops | bytes accessed | tf_op | source)
XLA Modules:
  0.0 144.0 jit_solution(3212266016706738339)
XLA Ops:
  0.6 125.3 %mlp_backward.1 = (bf16[2048,2048]{1,0:T(8,128)(2,1)}, bf16[2048,1024]{1,0:T(8,128)(2,1)}, bf16[2048,1024]{1,0:T(8,128)(2,1)}, bf16[1024,2048]{1,0:T(8,128)(2,1)}) custom-call(bf16[2048,2048]{1,0:T(8,128)(2,1)} %x_ref.1, bf16[2048,2048]{1,0:T(8,128)(2,1)} %dy_ref.1, bf16[2048,1024]{1,0:T(8,128)(2,1)} %gate_ref.1, bf16[2048,1024]{1,0:T(8,128)(2,1)} %up_ref.1, ...), custom_call_target="tpu_custom_call" | custom-call | tf_op jit(solution)/shard_map/mlp_backward/pallas_call | solution.py:296
  126.0 0.0 copy-start.2
  126.0 8.6 %copy.15 = bf16[2048,2048]{1,0:T(8,128)(2,1)} copy(bf16[2048,2048]{1,0:T(8,128)(2,1)} %get-tuple-element.8) | data formatting | bytes 16777216
  134.6 0.0 copy-done.2
  134.6 0.0 copy-start.1
  134.6 2.1 %copy.16 = bf16[2048,1024]{1,0:T(8,128)(2,1)} copy(bf16[2048,1024]{1,0:T(8,128)(2,1)S(1)} %copy-done.2) | data formatting | bytes 8388608
  136.7 1.6 %copy-done.1 = bf16[2048,1024]{1,0:T(8,128)(2,1)S(1)} copy-done((bf16[2048,1024]{1,0:T(8,128)(2,1)S(1)}, bf16[2048,1024]{1,0:T(8,128)(2,1)}, u32[]{:S(2)}) %copy-start.1) | copy-done | bytes 4194328
  138.3 0.0 copy-start
  138.3 2.1 %copy.17 = bf16[2048,1024]{1,0:T(8,128)(2,1)} copy(bf16[2048,1024]{1,0:T(8,128)(2,1)S(1)} %copy-done.1) | data formatting | bytes 8388608
  140.4 1.6 %copy-done = bf16[1024,2048]{1,0:T(8,128)(2,1)S(1)} copy-done((bf16[1024,2048]{1,0:T(8,128)(2,1)S(1)}, bf16[1024,2048]{1,0:T(8,128)(2,1)}, u32[]{:S(2)}) %copy-start) | copy-done | bytes 4194328
  142.0 2.0 %copy.18 = bf16[1024,2048]{1,0:T(8,128)(2,1)} copy(bf16[1024,2048]{1,0:T(8,128)(2,1)S(1)} %copy-done) | data formatting | bytes 8388608
Async XLA Ops:
  126.0 8.6 %copy-start.2 = (bf16[2048,1024]{1,0:T(8,128)(2,1)S(1)}, bf16[2048,1024]{1,0:T(8,128)(2,1)}, u32[]{:S(2)}) copy-start(bf16[2048,1024]{1,0:T(8,128)(2,1)} %get-tuple-element.9) | copy-start | bytes 12582916
  134.6 3.7 %copy-start.1 = (bf16[2048,1024]{1,0:T(8,128)(2,1)S(1)}, bf16[2048,1024]{1,0:T(8,128)(2,1)}, u32[]{:S(2)}) copy-start(bf16[2048,1024]{1,0:T(8,128)(2,1)} %get-tuple-element.10) | copy-start | bytes 12582916
  138.3 3.7 %copy-start = (bf16[1024,2048]{1,0:T(8,128)(2,1)S(1)}, bf16[1024,2048]{1,0:T(8,128)(2,1)}, u32[]{:S(2)}) copy-start(bf16[1024,2048]{1,0:T(8,128)(2,1)} %get-tuple-element.11) | copy-start | bytes 12582916

commit v2 on v0

v2 whole, which is shorter than its diff:
```python
import functools

import jax
import jax.numpy as jnp
from jax import lax
from jax.experimental import pallas as pl
from jax.experimental.pallas import tpu as pltpu
from jax.sharding import PartitionSpec as P

BF16, F32 = jnp.bfloat16, jnp.float32
MESH = pl.DeviceIdType.MESH
HALF = 1024
UNIT = 256
BIG, SMALL = 128, 64
KEPT = 5
NT = (((1,), (1,)), ((), ()))
NN = (((1,), (0,)), ((), ()))


def dot(a, b, dims):
    return lax.dot_general(a, b, dims, preferred_element_type=F32)


def span(i, n):
    return pl.ds(pl.multiple_of(i * n, n), n)


def kernel(
    x_ref, dy_ref, gate_ref, up_ref, wg_ref, wu_ref, wd_ref,
    dxa, dxb, dwg, dwu, dwd,
    dy, dg, du, hid, gu, own, stage, pt, rs, xb,
    wd_sem, w_sem, dy_sem, gu_sem, x_sem, pt_send, pt_recv,
    rs_send, rs_recv, q_send, q_recv, dd_send, dd_recv,
):
    rows, d = dy.shape
    units = rows // UNIT
    per = UNIT // BIG
    n_small = UNIT // SMALL
    n_big = (units - 2) * per
    chunks = 2 * n_small + n_big
    me = lax.axis_index("tp")
    z, c = me // 2, me % 2
    m = jnp.where(c == 1, z, 3 - z)
    first, last = m == 0, m == 3
    partner = z * 2 + 1 - c
    following = jnp.clip(z + 2 * c - 1, 0, 3) * 2 + c
    previous = jnp.clip(z - 2 * c + 1, 0, 3) * 2 + c
    mine = pl.multiple_of(c * HALF, HALF)
    other = pl.multiple_of((1 - c) * HALF, HALF)

    part = HALF // 2

    def load_wd(i):
        return pltpu.make_async_copy(wd_ref.at[span(i, part)], dwd.at[span(i, part)], wd_sem.at[i])

    def load_w(i):
        src, dst = ((wg_ref, dwg), (wu_ref, dwu))[i]
        return pltpu.make_async_copy(src, dst, w_sem.at[i])

    def load_dy(i):
        return pltpu.make_async_copy(dy_ref.at[span(i, UNIT)], dy.at[span(i, UNIT)], dy_sem.at[i])

    def load_gu(i, j):
        src = (gate_ref, up_ref)[j]
        slot = lax.rem(i, 2)
        return pltpu.make_async_copy(src.at[span(i, UNIT)], gu.at[slot, j], gu_sem.at[slot, j])

    def load_x(i):
        slot = lax.rem(i, 2)
        return pltpu.make_async_copy(x_ref.at[:, span(i, UNIT)], xb.at[slot], x_sem.at[slot])

    load_dy(0).start()
    load_wd(0).start()
    load_gu(0, 0).start()
    load_gu(0, 1).start()
    load_wd(1).start()
    load_w(0).start()
    load_w(1).start()
    load_gu(1, 0).start()
    load_gu(1, 1).start()
    for i in range(1, units):
        load_dy(i).start()
    load_x(0).start()
    load_x(1).start()

    barrier = pltpu.get_barrier_semaphore()
    pl.semaphore_signal(barrier, inc=1, device_id={"tp": partner}, device_id_type=MESH)

    @pl.when(m < 3)
    def _():
        pl.semaphore_signal(barrier, inc=1, device_id={"tp": following}, device_id_type=MESH)

    @pl.when(m > 0)
    def _():
        pl.semaphore_signal(barrier, inc=1, device_id={"tp": previous}, device_id_type=MESH)

    pl.semaphore_wait(barrier, jnp.where(first | last, 2, 3))

    def remote(src, dst, send, recv, device):
        return pltpu.make_async_remote_copy(
            src_ref=src, dst_ref=dst, send_sem=send, recv_sem=recv,
            device_id={"tp": device}, device_id_type=MESH)

    def to_partner(j):
        return remote(
            stage.at[span(lax.rem(j, 2 * per), BIG)], pt.at[span(j, BIG)], pt_send.at[j], pt_recv.at[j], partner)

    def pass_sum(k, r):
        return remote(pt.at[r], rs.at[r], rs_send.at[k], rs_recv.at[k], following)

    def turn(k, r):
        return remote(dxa.at[r], dxb.at[r], rs_send.at[k], q_recv.at[k], partner)

    def pass_result(k, r):
        return remote(dxb.at[r], dxb.at[r], q_send.at[k], q_recv.at[k], following)

    def share_result(k, r):
        return remote(dxb.at[r], dxa.at[r], dd_send.at[k], dd_recv.at[k], partner)

    def sum_step(k, r, o, wait_term):
        wait_term()

        @pl.when(first)
        def _():
            pt[r] = (own[o] + pt[r].astype(F32)).astype(BF16)

        @pl.when(m > 0)
        def _():
            pass_sum(k, r).wait_recv()

        @pl.when((m > 0) & (m < 3))
        def _():
            pt[r] = (own[o] + pt[r].astype(F32) + rs[r].astype(F32)).astype(BF16)

        @pl.when(m < 3)
        def _():
            pass_sum(k, r).start()

        @pl.when(last)
        def _():
            dxa[r] = (own[o] + pt[r].astype(F32) + rs[r].astype(F32)).astype(BF16)
            turn(k, r).start()

    def result_step(k, r):
        pass_result(k, r).wait_recv()

        @pl.when(m < 3)
        def _():
            pass_result(k, r).start()

        @pl.when(m > 0)
        def _():
            share_result(k, r).start()

    def drain_step(k, r):
        @pl.when(m < 3)
        def _():
            pass_sum(k, r).wait_send()
            pass_result(k, r).wait_send()
            share_result(k, r).wait_recv()

        @pl.when(last)
        def _():
            turn(k, r).wait_send()

        @pl.when(m > 0)
        def _():
            share_result(k, r).wait_send()

    tail = n_small + n_big

    def small_row(k):
        return jnp.where(k < n_small, k, k + n_big)

    def big_row(k):
        return k - n_small + per

    def small_loop(lo, hi, step):
        def body(k, _):
            step(k, SMALL, small_row(k))
            return 0

        lax.fori_loop(lo, hi, body, 0)

    def big_loop(lo, hi, step):
        def body(k, _):
            step(k, BIG, 2 * big_row(k))
            return 0

        lax.fori_loop(lo, hi, body, 0)

    def each(lo, hi, step):
        small_loop(jnp.minimum(lo, n_small), jnp.minimum(hi, n_small), step)
        big_loop(jnp.clip(lo, n_small, tail), jnp.clip(hi, n_small, tail), step)
        small_loop(jnp.maximum(lo, tail), jnp.maximum(hi, tail), step)

    def rows_of(n, at):
        return pl.ds(pl.multiple_of(at * SMALL, n), n)

    def do_sum(k, n, at):
        kept = lax.rem(at // n_small, KEPT) * n_small + lax.rem(at, n_small)

        def wait_term():
            @pl.when(lax.rem(at, 2) == 0)
            def _():
                to_partner(at // 2).wait_recv()

        sum_step(k, rows_of(n, at), rows_of(n, kept), wait_term)

    def do_result(k, n, at):
        result_step(k, rows_of(n, at))

    def do_drain(k, n, at):
        drain_step(k, rows_of(n, at))

    blocks = rows // SMALL

    def count(n):
        n = jnp.clip(n, 0, blocks)
        return jnp.where(
            n < n_small, n,
            jnp.where(n < blocks - n_small, n_small + (n - n_small) // 2, n - (blocks - n_small) + tail))

    def paced(s):
        return jnp.maximum((s - 2) * 8 - 20 * m + 7, 0) // 7

    def early(s):
        cap = n_small * ((s + 1) // 3)
        lead = jnp.where(s < 3, cap, n_small * (s // 3))
        floor = n_small * jnp.maximum((s + 2) // 3 - KEPT, 0)
        return count(jnp.where(first, lead, jnp.minimum(jnp.maximum(paced(s), floor), cap)))

    def late(s):
        n = paced(s)
        return count(jnp.where(first, blocks, n)), count(n - blocks)

    def serve_sums(s):
        each(early(s - 1), early(s), do_sum)

    def serve(s):
        s0, r0 = late(s - 1)
        s1, r1 = late(s)
        each(s0, s1, do_sum)
        each(r0, r1, do_result)

    n = HALF // 2

    def unit(u, _):
        r = span(u, UNIT)
        slot = lax.rem(u, 2)
        load_dy(u).wait()
        for b in range(2):
            f = slice(b * n, (b + 1) * n)

            @pl.when(u == 0)
            def _():
                load_wd(b).wait()
                if b == 0:
                    load_gu(u, 0).wait()
                    load_gu(u, 1).wait()

            if b == 0:
                @pl.when(u > 0)
                def _():
                    load_gu(u, 0).wait()
                    load_gu(u, 1).wait()

            dh = dot(dy[r, :], dwd[f, :], NT)
            gate = gu[slot, 0, :, f].astype(F32)
            up = gu[slot, 1, :, f].astype(F32)
            sig = jax.nn.sigmoid(gate)
            silu = gate * sig
            hid[r, f] = (silu * up).astype(BF16)
            du[r, f] = (dh * silu).astype(BF16)
            dg[r, f] = ((dh * up) * (sig * (1.0 + gate * (1.0 - sig)))).astype(BF16)

        @pl.when(u + 2 < units)
        def _():
            load_gu(u + 2, 0).start()
            load_gu(u + 2, 1).start()

        serve_sums(3 * u)

        @pl.when(u == 0)
        def _():
            load_w(0).wait()
            load_w(1).wait()

        @pl.when(u >= 2)
        def _():
            for j in range(per):
                to_partner((u - 2) * per + j).wait_send()

        stage[span(slot, UNIT)] = (
            dot(dg[r], dwg[pl.ds(other, HALF), :], NT) + dot(du[r], dwu[pl.ds(other, HALF), :], NT)
        ).astype(BF16)
        for j in range(per):
            to_partner(u * per + j).start()
        serve_sums(3 * u + 1)
        own[span(lax.rem(u, KEPT), UNIT)] = dot(dg[r], dwg[pl.ds(mine, HALF), :], NT) + dot(du[r], dwu[pl.ds(mine, HALF), :], NT)
        serve_sums(3 * u + 2)
        return 0

    lax.fori_loop(0, units, unit, 0)

    slots = 3 * units
    each(early(slots - 1), late(slots - 1)[0], do_sum)
    halves = d // HALF
    n_down = halves * HALF // UNIT

    def down(i, _):
        left = hid[:, span(i // halves, UNIT)].T
        at = span(lax.rem(i, halves), HALF)
        dwd[span(i // halves, UNIT), at] = dot(left, dy[:, at], NN).astype(BF16)
        serve(slots + i)
        return 0

    lax.fori_loop(0, n_down, down, 0)
    n_side = d // UNIT

    def side(i, _):
        slot = lax.rem(i, 2)
        s = slots + n_down + 2 * i
        load_x(i).wait()
        left = xb[slot].T
        dwg[span(i, UNIT), :] = dot(left, dg[...], NN).astype(BF16)
        serve(s)
        left = xb[slot].T
        dwu[span(i, UNIT), :] = dot(left, du[...], NN).astype(BF16)

        @pl.when(i + 2 < n_side)
        def _():
            load_x(i + 2).start()

        serve(s + 1)
        return 0

    lax.fori_loop(0, n_side, side, 0)
    s0, r0 = late(slots + n_down + 2 * n_side - 1)
    each(s0, chunks, do_sum)
    each(r0, chunks, do_result)

    each(0, chunks, do_drain)

    def sent(j, _):
        to_partner(j).wait_send()
        return 0

    lax.fori_loop((units - 2) * per, units * per, sent, 0)


def write_out(dxa, dxb, dwg, dwu, dwd, dx_ref, dwg_ref, dwu_ref, dwd_ref, sem):
    c = lax.axis_index("tp") % 2
    mine = pl.multiple_of(c * HALF, HALF)
    other = pl.multiple_of((1 - c) * HALF, HALF)
    copies = [
        pltpu.make_async_copy(src, dst, sem.at[i])
        for i, (src, dst) in enumerate((
            (dxa, dx_ref.at[:, pl.ds(mine, HALF)]),
            (dxb, dx_ref.at[:, pl.ds(other, HALF)]),
            (dwg, dwg_ref), (dwu, dwu_ref), (dwd, dwd_ref)))
    ]
    for copy in copies:
        copy.start()
    for copy in copies:
        copy.wait()


def backward(x, dy, gate, up, w_gate, w_up, w_down):
    rows, d = x.shape
    ff = w_down.shape[0]
    units = rows // UNIT
    chunks = 2 * (UNIT // SMALL) + (units - 2) * (UNIT // BIG)
    hbm = pl.BlockSpec(memory_space=pltpu.HBM)
    vmem = pl.BlockSpec(memory_space=pltpu.VMEM)
    dma = pltpu.SemaphoreType.DMA
    half = pltpu.VMEM((rows, HALF), BF16)
    parts = pl.pallas_call(
        kernel,
        out_shape=[
            pltpu.VMEM((rows, HALF), BF16), pltpu.VMEM((rows, HALF), BF16),
            pltpu.VMEM((d, ff), BF16), pltpu.VMEM((d, ff), BF16), pltpu.VMEM((ff, d), BF16),
        ],
        in_specs=[hbm] * 7,
        out_specs=[vmem] * 5,
        scratch_shapes=[
            pltpu.VMEM((rows, d), BF16),
            half, half, half,
            pltpu.VMEM((2, 2, UNIT, ff), BF16),
            pltpu.VMEM((KEPT * UNIT, HALF), F32),
            pltpu.VMEM((2 * UNIT, HALF), BF16),
            half, half,
            pltpu.VMEM((2, rows, UNIT), BF16),
            dma((2,)), dma((2,)), dma((units,)), dma((2, 2)), dma((2,)),
            dma((rows // BIG,)), dma((rows // BIG,)),
        ] + [dma((chunks,))] * 6,
        compiler_params=pltpu.CompilerParams(
            collective_id=0, has_side_effects=True, vmem_limit_bytes=43 * 2**20),
        name="mlp_backward",
    )(x, dy, gate, up, w_gate, w_up, w_down)
    return pl.pallas_call(
        write_out,
        out_shape=[
            jax.ShapeDtypeStruct((rows, d), BF16),
            jax.ShapeDtypeStruct((d, ff), BF16),
            jax.ShapeDtypeStruct((d, ff), BF16),
            jax.ShapeDtypeStruct((ff, d), BF16),
        ],
        in_specs=[vmem] * 5,
        out_specs=[hbm] * 4,
        scratch_shapes=[dma((5,))],
        compiler_params=pltpu.CompilerParams(vmem_limit_bytes=2**20),
        name="write_out",
    )(*parts)


def solution(mesh):
    tokens, columns, rows = P("dp", None), P(None, "tp"), P("tp", None)
    return jax.shard_map(
        backward,
        mesh=mesh,
        in_specs=(tokens, tokens, P("dp", "tp"), P("dp", "tp"), columns, columns, rows),
        out_specs=(tokens, P("dp", "tp"), P("dp", "tp"), P(("dp", "tp"), None)),
        check_vma=False,
    )
```

time: 254 us -> 129 us (0.51)
  Pallas kernels: 0 us -> 129 us
  waiting for transfers between devices: 119 us -> 0 us
  matrix products: 99.1 us -> 0 us
  local copies, waits for them, and re-layouts: 21.2 us -> 0 us
  between operations: 14 us -> 0.64 us
    pallas_call x0 -> x2, Pallas kernels: none -> 129 us  [the longest x1 121 us: backward(): pl.pallas_call(kernel, out_shape=[pltpu.VMEM((rows, HALF), BF16), pltpu.V...]
    psum x1 -> x0, waiting for transfers between devices: 119 us -> none  [step(): dx = lax.psum(term.astype(jnp.bfloat16), 'tp')]
    dot_general x6 -> x0, matrix products: 99.1 us -> none  [the longest x1 20.5 us: step(): jnp.dot(d_up, w_up.T, preferred_element_type=jnp.float32)]
    unnamed x7 -> x0, local copies, waits for them, and re-layouts: 21.2 us -> none
  transfers between devices with their start and end apart: 1 -> 0, of which waited for: 1 -> 0; matrix products, arithmetic and copies ran while one was open for 23% -> 0% of each run, Pallas kernels for 0% -> 0%
where the time goes in v2:
time: 129 us
  Pallas kernels  129 us (100%)
    pallas_call x1, Pallas kernels, backward(): pl.pallas_call(kernel, out_shape=[pltpu.VMEM((rows, HALF), BF16), pltpu.V...  121 us
    pallas_call x1, Pallas kernels, backward(): pl.pallas_call(write_out, out_shape=[jax.ShapeDtypeStruct((rows, d), BF16...  7.23 us

profile of v2, /device:TPU:0, one launch (start us, length us, event | category | flops | bytes accessed | tf_op | source)
XLA Modules:
  0.0 129.3 jit_solution(6938598616195108371)
XLA Ops:
  0.6 121.4 %mlp_backward.1 = (bf16[2048,1024]{1,0:T(8,128)(2,1)S(1)}, bf16[2048,1024]{1,0:T(8,128)(2,1)S(1)}, bf16[2048,1024]{1,0:T(8,128)(2,1)S(1)}, bf16[2048,1024]{1,0:T(8,128)(2,1)S(1)}, bf16[1024,2048]{1,0:T(8,128)(2,1)S(1)}) custom-call(bf16[2048,2048]{1,0:T(8,128)(2,1)} %x_ref.1, bf16[2048,2048]{1,0:T(8,128)(2,1)} %dy_ref.1, bf16[2048,1024]{1,0:T(8,128)(2,1)} %gate_ref.1, ...), custom_call_target="tpu_custom_call" | custom-call | tf_op jit(solution)/shard_map/mlp_backward/pallas_call | solution.py:378
  122.1 7.2 %write_out.1 = (bf16[2048,2048]{1,0:T(8,128)(2,1)}, bf16[2048,1024]{1,0:T(8,128)(2,1)}, bf16[2048,1024]{1,0:T(8,128)(2,1)}, bf16[1024,2048]{1,0:T(8,128)(2,1)}) custom-call(bf16[2048,1024]{1,0:T(8,128)(2,1)S(1)} %get-tuple-element.9.dxa, bf16[2048,1024]{1,0:T(8,128)(2,1)S(1)} %get-tuple-element.10.dxb, bf16[2048,1024]{1,0:T(8,128)(2,1)S(1)} %get-tuple-element.11.dwg, ...), custom_call_target="tpu_custom_call" | custom-call | tf_op jit(solution)/shard_map/write_out/pallas_call | solution.py:401

commit v3 on v0

v3 whole, which is shorter than its diff:
```python
import jax
import jax.numpy as jnp
from jax import lax
from jax.experimental import pallas as pl
from jax.experimental.pallas import tpu as pltpu
from jax.sharding import PartitionSpec as P

BF16, F32 = jnp.bfloat16, jnp.float32
MESH = pl.DeviceIdType.MESH
HALF = 1024
UNIT = 256
ROWS, COLS = 128, 512
PER = 4
KEPT = 5
TICKS = (5, 7, 9, 11, 13)
NT = (((1,), (1,)), ((), ()))
NN = (((1,), (0,)), ((), ()))


def dot(a, b, dims):
    return lax.dot_general(a, b, dims, preferred_element_type=F32)


def span(i, n):
    return pl.ds(pl.multiple_of(i * n, n), n)


def kernel(
    x_ref, dy_ref, gate_ref, up_ref, wg_ref, wu_ref, wd_ref,
    dxa, dxb, dwg, dwu, dwd,
    dy, dg, du, hid, gu, own, stage, pt, rs, xb,
    wd_sem, w_sem, dy_sem, gu_sem, x_sem,
    pt_send, pt_recv, rs_send, rs_recv, q_send, q_recv, dd_send, dd_recv,
):
    rows, d = dy.shape
    units = rows // UNIT
    chunks = units * PER
    me = lax.axis_index("tp")
    z, c = me // 2, me % 2
    m = jnp.where(c == 1, z, 3 - z)
    first, last = m == 0, m == 3
    partner = z * 2 + 1 - c
    following = jnp.clip(z + 2 * c - 1, 0, 3) * 2 + c
    previous = jnp.clip(z - 2 * c + 1, 0, 3) * 2 + c
    mine, other = c * (HALF // COLS), (1 - c) * (HALF // COLS)

    def load_wd(i):
        return pltpu.make_async_copy(wd_ref.at[span(i, COLS)], dwd.at[span(i, COLS)], wd_sem.at[i])

    def load_w(i):
        at = span((other, mine)[i % 2] + i // 2, COLS)
        return [
            pltpu.make_async_copy(src.at[at], dst.at[at], w_sem.at[i, j])
            for j, (src, dst) in enumerate(((wg_ref, dwg), (wu_ref, dwu)))
        ]

    def load_dy(i):
        return pltpu.make_async_copy(dy_ref.at[span(i, UNIT)], dy.at[span(i, UNIT)], dy_sem.at[i])

    def load_gu(i):
        slot = lax.rem(i, 2)
        return [
            pltpu.make_async_copy(src.at[span(i, UNIT)], gu.at[slot, j], gu_sem.at[slot, j])
            for j, src in enumerate((gate_ref, up_ref))
        ]

    def load_x(i):
        slot = lax.rem(i, 2)
        return pltpu.make_async_copy(x_ref.at[:, span(i, UNIT)], xb.at[slot], x_sem.at[slot])

    def start(copies):
        for copy in copies:
            copy.start()

    def wait(copies):
        for copy in copies:
            copy.wait()

    start(load_gu(0))
    start([load_dy(0), load_wd(0), load_wd(1)])
    start(load_w(0) + load_w(1) + load_w(2) + load_w(3) + load_gu(1))
    start([load_dy(i) for i in range(1, units)])
    start([load_x(0), load_x(1)])

    barrier = pltpu.get_barrier_semaphore()
    pl.semaphore_signal(barrier, inc=1, device_id={"tp": partner}, device_id_type=MESH)

    @pl.when(m < 3)
    def _():
        pl.semaphore_signal(barrier, inc=1, device_id={"tp": following}, device_id_type=MESH)

    @pl.when(m > 0)
    def _():
        pl.semaphore_signal(barrier, inc=1, device_id={"tp": previous}, device_id_type=MESH)

    pl.semaphore_wait(barrier, jnp.where(first | last, 2, 3))

    def place(k, ring=0):
        u = k // PER
        if ring:
            u = lax.rem(u, ring)
        return span(u * (UNIT // ROWS) + lax.rem(k, 2), ROWS), span(lax.rem(k, PER) // 2, COLS)

    def remote(src, dst, send, recv, device):
        return pltpu.make_async_remote_copy(
            src_ref=src, dst_ref=dst, send_sem=send, recv_sem=recv,
            device_id={"tp": device}, device_id_type=MESH)

    def to_partner(k):
        return remote(stage.at[place(k, 2)], pt.at[place(k)], pt_send.at[k], pt_recv.at[k], partner)

    def pass_sum(k):
        return remote(pt.at[place(k)], rs.at[place(k)], rs_send.at[k], rs_recv.at[k], following)

    def turn(k):
        return remote(dxa.at[place(k)], dxb.at[place(k)], rs_send.at[k], q_recv.at[k], partner)

    def pass_result(k):
        return remote(dxb.at[place(k)], dxb.at[place(k)], q_send.at[k], q_recv.at[k], following)

    def share_result(k):
        return remote(dxb.at[place(k)], dxa.at[place(k)], dd_send.at[k], dd_recv.at[k], partner)

    def sum_step(k, _):
        at, kept = place(k), place(k, KEPT)
        to_partner(k).wait_recv()

        @pl.when(first)
        def _():
            pt[at] = (own[kept] + pt[at].astype(F32)).astype(BF16)

        @pl.when(m > 0)
        def _():
            pass_sum(k).wait_recv()

        @pl.when((m > 0) & (m < 3))
        def _():
            pt[at] = (own[kept] + pt[at].astype(F32) + rs[at].astype(F32)).astype(BF16)

        @pl.when(m < 3)
        def _():
            pass_sum(k).start()

        @pl.when(last)
        def _():
            dxa[at] = (own[kept] + pt[at].astype(F32) + rs[at].astype(F32)).astype(BF16)
            turn(k).start()

        return 0

    def result_step(k, _):
        pass_result(k).wait_recv()

        @pl.when(m < 3)
        def _():
            pass_result(k).start()

        @pl.when(m > 0)
        def _():
            share_result(k).start()

        return 0

    def serve(done, upto, step):
        upto = jnp.maximum(done, jnp.minimum(upto, chunks))
        lax.fori_loop(done, upto, step, 0)
        return upto

    def paced(tick):
        return jnp.maximum((tick - 8 - 10 * m) * 8 + 25, 0) // 25

    def serve_sums(done, u, sub):
        ready = PER * u + (0, 0, 2, 2, 4)[sub]
        lead = PER * u + (0, 0, 0, 2, 2)[sub]
        needed = PER * jnp.maximum(u - KEPT + (sub >= 1), 0)
        n = jnp.minimum(jnp.maximum(paced(13 * u + TICKS[sub]), needed), ready)
        return serve(done, jnp.where(first, lead, n), sum_step)

    parts = [slice(i * COLS, (i + 1) * COLS) for i in range(HALF // COLS)]

    def unit(u, done):
        r = span(u, UNIT)
        slot = lax.rem(u, 2)
        load_dy(u).wait()
        wait(load_gu(u))
        for b, f in enumerate(parts):
            @pl.when(u == 0)
            def _():
                load_wd(b).wait()

            dh = dot(dy[r, :], dwd[f, :], NT)
            gate = gu[slot, 0, :, f].astype(F32)
            up = gu[slot, 1, :, f].astype(F32)
            sig = jax.nn.sigmoid(gate)
            silu = gate * sig
            hid[r, f] = (silu * up).astype(BF16)
            du[r, f] = (dh * silu).astype(BF16)
            dg[r, f] = ((dh * up) * (sig * (1.0 + gate * (1.0 - sig)))).astype(BF16)

        @pl.when(u + 2 < units)
        def _():
            start(load_gu(u + 2))

        done = serve_sums(done, u, 0)

        @pl.when(u >= 2)
        def _():
            for j in range(PER):
                to_partner((u - 2) * PER + j).wait_send()

        for b, f in enumerate(parts):
            @pl.when(u == 0)
            def _():
                wait(load_w(2 * b))

            at = span(other + b, COLS)
            stage[span(lax.rem(u, 2), UNIT), f] = (dot(dg[r], dwg[at, :], NT) + dot(du[r], dwu[at, :], NT)).astype(BF16)
            for j in range(2):
                to_partner(u * PER + 2 * b + j).start()
            done = serve_sums(done, u, 1 + 2 * b)

            @pl.when(u == 0)
            def _():
                wait(load_w(2 * b + 1))

            at = span(mine + b, COLS)
            own[span(lax.rem(u, KEPT), UNIT), f] = dot(dg[r], dwg[at, :], NT) + dot(du[r], dwu[at, :], NT)
            done = serve_sums(done, u, 2 + 2 * b)
        return done

    done = lax.fori_loop(0, units, unit, jnp.int32(0))

    def serve_both(state, tick):
        n = paced(tick)
        sums = serve(state[0], jnp.where(first, chunks, n), sum_step)
        return sums, serve(state[1], n - chunks, result_step)

    ticks = 13 * units
    halves = d // HALF
    n_down = halves * HALF // UNIT
    n_side = d // UNIT

    def down(i, state):
        for j in range(2):
            at = span(2 * lax.rem(i, halves) + j, COLS)
            left = hid[:, span(i // halves, UNIT)].T
            dwd[span(i // halves, UNIT), at] = dot(left, dy[:, at], NN).astype(BF16)
            state = serve_both(state, ticks + 4 * i + 2 * j + 2)
        return state

    state = lax.fori_loop(0, n_down, down, (done, jnp.int32(0)))
    ticks += 4 * n_down

    def side(i, state):
        slot = lax.rem(i, 2)
        load_x(i).wait()
        for j, (right, out) in enumerate(((dg, dwg), (du, dwu))):
            for b, f in enumerate(parts):
                left = xb[slot].T
                out[span(i, UNIT), f] = dot(left, right[:, f], NN).astype(BF16)
                if j + b == 2:
                    @pl.when(i + 2 < n_side)
                    def _():
                        load_x(i + 2).start()

                state = serve_both(state, ticks + 8 * i + 4 * j + 2 * b + 2)
        return state

    state = lax.fori_loop(0, n_side, side, state)
    serve(state[0], chunks, sum_step)
    serve(state[1], chunks, result_step)

    def drain(k, _):
        @pl.when(m < 3)
        def _():
            pass_sum(k).wait_send()
            pass_result(k).wait_send()
            share_result(k).wait_recv()

        @pl.when(last)
        def _():
            turn(k).wait_send()

        @pl.when(m > 0)
        def _():
            share_result(k).wait_send()

        return 0

    lax.fori_loop(0, chunks, drain, 0)

    def sent(k, _):
        to_partner(k).wait_send()
        return 0

    lax.fori_loop((units - 2) * PER, chunks, sent, 0)


def write_out(dxa, dxb, dwg, dwu, dwd, dx_ref, dwg_ref, dwu_ref, dwd_ref, sem):
    c = lax.axis_index("tp") % 2
    copies = [
        pltpu.make_async_copy(src, dst, sem.at[i])
        for i, (src, dst) in enumerate((
            (dxa, dx_ref.at[:, span(c, HALF)]),
            (dxb, dx_ref.at[:, span(1 - c, HALF)]),
            (dwg, dwg_ref), (dwu, dwu_ref), (dwd, dwd_ref)))
    ]
    for copy in copies:
        copy.start()
    for copy in copies:
        copy.wait()


def backward(x, dy, gate, up, w_gate, w_up, w_down):
    rows, d = x.shape
    ff = w_down.shape[0]
    units = rows // UNIT
    chunks = units * PER
    hbm = pl.BlockSpec(memory_space=pltpu.HBM)
    vmem = pl.BlockSpec(memory_space=pltpu.VMEM)
    dma = pltpu.SemaphoreType.DMA
    half = pltpu.VMEM((rows, HALF), BF16)
    results = pl.pallas_call(
        kernel,
        out_shape=[
            pltpu.VMEM((rows, HALF), BF16), pltpu.VMEM((rows, HALF), BF16),
            pltpu.VMEM((d, ff), BF16), pltpu.VMEM((d, ff), BF16), pltpu.VMEM((ff, d), BF16),
        ],
        in_specs=[hbm] * 7,
        out_specs=[vmem] * 5,
        scratch_shapes=[
            pltpu.VMEM((rows, d), BF16),
            half, half, half,
            pltpu.VMEM((2, 2, UNIT, ff), BF16),
            pltpu.VMEM((KEPT * UNIT, HALF), F32),
            pltpu.VMEM((2 * UNIT, HALF), BF16),
            half, half,
            pltpu.VMEM((2, rows, UNIT), BF16),
            dma((2,)), dma((4, 2)), dma((units,)), dma((2, 2)), dma((2,)),
        ] + [dma((chunks,))] * 8,
        compiler_params=pltpu.CompilerParams(
            collective_id=0, has_side_effects=True, vmem_limit_bytes=67043328 - 20 * 2**20),
        name="mlp_backward",
    )(x, dy, gate, up, w_gate, w_up, w_down)
    return pl.pallas_call(
        write_out,
        out_shape=[
            jax.ShapeDtypeStruct((rows, d), BF16),
            jax.ShapeDtypeStruct((d, ff), BF16),
            jax.ShapeDtypeStruct((d, ff), BF16),
            jax.ShapeDtypeStruct((ff, d), BF16),
        ],
        in_specs=[vmem] * 5,
        out_specs=[hbm] * 4,
        scratch_shapes=[dma((5,))],
        compiler_params=pltpu.CompilerParams(vmem_limit_bytes=2**20),
        name="write_out",
    )(*results)


def solution(mesh):
    tokens, columns, rows = P("dp", None), P(None, "tp"), P("tp", None)
    return jax.shard_map(
        backward,
        mesh=mesh,
        in_specs=(tokens, tokens, P("dp", "tp"), P("dp", "tp"), columns, columns, rows),
        out_specs=(tokens, P("dp", "tp"), P("dp", "tp"), P(("dp", "tp"), None)),
        check_vma=False,
    )
```

time: 254 us -> 128 us (0.50)
  Pallas kernels: 0 us -> 127 us
  waiting for transfers between devices: 119 us -> 0 us
  matrix products: 99.1 us -> 0 us
  local copies, waits for them, and re-layouts: 21.2 us -> 0 us
  between operations: 14 us -> 0.64 us
    pallas_call x0 -> x2, Pallas kernels: none -> 127 us  [the longest x1 120 us: backward(): pl.pallas_call(kernel, out_shape=[pltpu.VMEM((rows, HALF), BF16), pltpu.V...]
    psum x1 -> x0, waiting for transfers between devices: 119 us -> none  [step(): dx = lax.psum(term.astype(jnp.bfloat16), 'tp')]
    dot_general x6 -> x0, matrix products: 99.1 us -> none  [the longest x1 20.5 us: step(): jnp.dot(d_up, w_up.T, preferred_element_type=jnp.float32)]
    unnamed x7 -> x0, local copies, waits for them, and re-layouts: 21.2 us -> none
  transfers between devices with their start and end apart: 1 -> 0, of which waited for: 1 -> 0; matrix products, arithmetic and copies ran while one was open for 23% -> 0% of each run, Pallas kernels for 0% -> 0%
where the time goes in v3:
time: 128 us
  Pallas kernels  127 us (99%)
    pallas_call x1, Pallas kernels, backward(): pl.pallas_call(kernel, out_shape=[pltpu.VMEM((rows, HALF), BF16), pltpu.V...  120 us
    pallas_call x1, Pallas kernels, backward(): pl.pallas_call(write_out, out_shape=[jax.ShapeDtypeStruct((rows, d), BF16...  7.23 us

profile of v3, /device:TPU:0, one launch (start us, length us, event | category | flops | bytes accessed | tf_op | source)
XLA Modules:
  0.0 127.7 jit_solution(11130228311344959222)
XLA Ops:
  0.6 119.9 %mlp_backward.1 = (bf16[2048,1024]{1,0:T(8,128)(2,1)S(1)}, bf16[2048,1024]{1,0:T(8,128)(2,1)S(1)}, bf16[2048,1024]{1,0:T(8,128)(2,1)S(1)}, bf16[2048,1024]{1,0:T(8,128)(2,1)S(1)}, bf16[1024,2048]{1,0:T(8,128)(2,1)S(1)}) custom-call(bf16[2048,2048]{1,0:T(8,128)(2,1)} %x_ref.1, bf16[2048,2048]{1,0:T(8,128)(2,1)} %dy_ref.1, bf16[2048,1024]{1,0:T(8,128)(2,1)} %gate_ref.1, ...), custom_call_target="tpu_custom_call" | custom-call | tf_op jit(solution)/shard_map/mlp_backward/pallas_call | solution.py:323
  120.5 7.2 %write_out.1 = (bf16[2048,2048]{1,0:T(8,128)(2,1)}, bf16[2048,1024]{1,0:T(8,128)(2,1)}, bf16[2048,1024]{1,0:T(8,128)(2,1)}, bf16[1024,2048]{1,0:T(8,128)(2,1)}) custom-call(bf16[2048,1024]{1,0:T(8,128)(2,1)S(1)} %get-tuple-element.9.dxa, bf16[2048,1024]{1,0:T(8,128)(2,1)S(1)} %get-tuple-element.10.dxb, bf16[2048,1024]{1,0:T(8,128)(2,1)S(1)} %get-tuple-element.11.dwg, ...), custom_call_target="tpu_custom_call" | custom-call | tf_op jit(solution)/shard_map/write_out/pallas_call | solution.py:345

commit v4 on v3

--- a/solution.py
+++ b/solution.py
@@ -12,7 +12,7 @@
 ROWS, COLS = 128, 512
 PER = 4
 KEPT = 5
-TICKS = (5, 7, 9, 11, 13)
+TICKS = (5, 9, 13)
 NT = (((1,), (1,)), ((), ()))
 NN = (((1,), (0,)), ((), ()))
 
@@ -42,13 +42,13 @@
     partner = z * 2 + 1 - c
     following = jnp.clip(z + 2 * c - 1, 0, 3) * 2 + c
     previous = jnp.clip(z - 2 * c + 1, 0, 3) * 2 + c
-    mine, other = c * (HALF // COLS), (1 - c) * (HALF // COLS)
+    mine, other = c, 1 - c
 
     def load_wd(i):
         return pltpu.make_async_copy(wd_ref.at[span(i, COLS)], dwd.at[span(i, COLS)], wd_sem.at[i])
 
     def load_w(i):
-        at = span((other, mine)[i % 2] + i // 2, COLS)
+        at = span((other, mine)[i], HALF)
         return [
             pltpu.make_async_copy(src.at[at], dst.at[at], w_sem.at[i, j])
             for j, (src, dst) in enumerate(((wg_ref, dwg), (wu_ref, dwu)))
@@ -78,7 +78,7 @@
 
     start(load_gu(0))
     start([load_dy(0), load_wd(0), load_wd(1)])
-    start(load_w(0) + load_w(1) + load_w(2) + load_w(3) + load_gu(1))
+    start(load_w(0) + load_w(1) + load_gu(1))
     start([load_dy(i) for i in range(1, units)])
     start([load_x(0), load_x(1)])
 
@@ -107,19 +107,24 @@
             device_id={"tp": device}, device_id_type=MESH)
 
     def to_partner(k):
-        return remote(stage.at[place(k, 2)], pt.at[place(k)], pt_send.at[k], pt_recv.at[k], partner)
+        return remote(stage.at[place(k, 2)], pt.at[place(k)], pt_send.at[lax.rem(k // PER, 2)], pt_recv.at[k], partner)
 
     def pass_sum(k):
-        return remote(pt.at[place(k)], rs.at[place(k)], rs_send.at[k], rs_recv.at[k], following)
+        return remote(pt.at[place(k)], rs.at[place(k)], rs_send, rs_recv.at[k], following)
 
     def turn(k):
-        return remote(dxa.at[place(k)], dxb.at[place(k)], rs_send.at[k], q_recv.at[k], partner)
+        return remote(dxa.at[place(k)], dxb.at[place(k)], rs_send, q_recv.at[k], partner)
 
     def pass_result(k):
-        return remote(dxb.at[place(k)], dxb.at[place(k)], q_send.at[k], q_recv.at[k], following)
+        return remote(dxb.at[place(k)], dxb.at[place(k)], q_send, q_recv.at[k], following)
 
     def share_result(k):
-        return remote(dxb.at[place(k)], dxa.at[place(k)], dd_send.at[k], dd_recv.at[k], partner)
+        return remote(dxb.at[place(k)], dxa.at[place(k)], dd_send, dd_recv, partner)
+
+    def unit_sent(u):
+        r = span(u, UNIT)
+        return remote(
+            stage.at[span(lax.rem(u, 2), UNIT)], pt.at[r], pt_send.at[lax.rem(u, 2)], pt_recv.at[0], partner)
 
     def sum_step(k, _):
         at, kept = place(k), place(k, KEPT)
@@ -167,14 +172,13 @@
         return upto
 
     def paced(tick):
-        return jnp.maximum((tick - 8 - 10 * m) * 8 + 25, 0) // 25
+        return jnp.maximum((tick - 8 - 14 * m) * 9 + 25, 0) // 25
 
     def serve_sums(done, u, sub):
-        ready = PER * u + (0, 0, 2, 2, 4)[sub]
-        lead = PER * u + (0, 0, 0, 2, 2)[sub]
+        ready = PER * (u + (sub == 2))
         needed = PER * jnp.maximum(u - KEPT + (sub >= 1), 0)
         n = jnp.minimum(jnp.maximum(paced(13 * u + TICKS[sub]), needed), ready)
-        return serve(done, jnp.where(first, lead, n), sum_step)
+        return serve(done, jnp.where(first, ready, n), sum_step)
 
     parts = [slice(i * COLS, (i + 1) * COLS) for i in range(HALF // COLS)]
 
@@ -205,27 +209,25 @@
 
         @pl.when(u >= 2)
         def _():
-            for j in range(PER):
-                to_partner((u - 2) * PER + j).wait_send()
-
-        for b, f in enumerate(parts):
-            @pl.when(u == 0)
-            def _():
-                wait(load_w(2 * b))
-
-            at = span(other + b, COLS)
-            stage[span(lax.rem(u, 2), UNIT), f] = (dot(dg[r], dwg[at, :], NT) + dot(du[r], dwu[at, :], NT)).astype(BF16)
-            for j in range(2):
-                to_partner(u * PER + 2 * b + j).start()
-            done = serve_sums(done, u, 1 + 2 * b)
-
-            @pl.when(u == 0)
-            def _():
-                wait(load_w(2 * b + 1))
-
-            at = span(mine + b, COLS)
-            own[span(lax.rem(u, KEPT), UNIT), f] = dot(dg[r], dwg[at, :], NT) + dot(du[r], dwu[at, :], NT)
-            done = serve_sums(done, u, 2 + 2 * b)
+            unit_sent(u - 2).wait_send()
+
+        @pl.when(u == 0)
+        def _():
+            wait(load_w(0))
+
+        at = span(other, HALF)
+        stage[span(lax.rem(u, 2), UNIT), :] = (dot(dg[r], dwg[at, :], NT) + dot(du[r], dwu[at, :], NT)).astype(BF16)
+        for j in range(PER):
+            to_partner(u * PER + j).start()
+        done = serve_sums(done, u, 1)
+
+        @pl.when(u == 0)
+        def _():
+            wait(load_w(1))
+
+        at = span(mine, HALF)
+        own[span(lax.rem(u, KEPT), UNIT), :] = dot(dg[r], dwg[at, :], NT) + dot(du[r], dwu[at, :], NT)
+        done = serve_sums(done, u, 2)
         return done
 
     done = lax.fori_loop(0, units, unit, jnp.int32(0))
@@ -241,11 +243,10 @@
     n_side = d // UNIT
 
     def down(i, state):
-        for j in range(2):
-            at = span(2 * lax.rem(i, halves) + j, COLS)
-            left = hid[:, span(i // halves, UNIT)].T
-            dwd[span(i // halves, UNIT), at] = dot(left, dy[:, at], NN).astype(BF16)
-            state = serve_both(state, ticks + 4 * i + 2 * j + 2)
+        at = span(lax.rem(i, halves), HALF)
+        left = hid[:, span(i // halves, UNIT)].T
+        dwd[span(i // halves, UNIT), at] = dot(left, dy[:, at], NN).astype(BF16)
+        state = serve_both(state, ticks + 4 * i + 4)
         return state
 
     state = lax.fori_loop(0, n_down, down, (done, jnp.int32(0)))
@@ -255,45 +256,33 @@
         slot = lax.rem(i, 2)
         load_x(i).wait()
         for j, (right, out) in enumerate(((dg, dwg), (du, dwu))):
-            for b, f in enumerate(parts):
-                left = xb[slot].T
-                out[span(i, UNIT), f] = dot(left, right[:, f], NN).astype(BF16)
-                if j + b == 2:
-                    @pl.when(i + 2 < n_side)
-                    def _():
-                        load_x(i + 2).start()
-
-                state = serve_both(state, ticks + 8 * i + 4 * j + 2 * b + 2)
+            left = xb[slot].T
+            out[span(i, UNIT), :] = dot(left, right[...], NN).astype(BF16)
+            if j == 1:
+                @pl.when(i + 2 < n_side)
+                def _():
+                    load_x(i + 2).start()
+
+            state = serve_both(state, ticks + 8 * i + 4 * j + 4)
         return state
 
     state = lax.fori_loop(0, n_side, side, state)
     serve(state[0], chunks, sum_step)
     serve(state[1], chunks, result_step)
 
-    def drain(k, _):
-        @pl.when(m < 3)
-        def _():
-            pass_sum(k).wait_send()
-            pass_result(k).wait_send()
-            share_result(k).wait_recv()
-
-        @pl.when(last)
-        def _():
-            turn(k).wait_send()
-
-        @pl.when(m > 0)
-        def _():
-            share_result(k).wait_send()
-
-        return 0
-
-    lax.fori_loop(0, chunks, drain, 0)
-
-    def sent(k, _):
-        to_partner(k).wait_send()
-        return 0
-
-    lax.fori_loop((units - 2) * PER, chunks, sent, 0)
+    remote(dxa, dxb, rs_send, rs_recv.at[0], partner).wait_send()
+
+    @pl.when(m < 3)
+    def _():
+        remote(dxb, dxb, q_send, q_recv.at[0], following).wait_send()
+        remote(dxb, dxa, dd_send, dd_recv, partner).wait_recv()
+
+    @pl.when(m > 0)
+    def _():
+        remote(dxb, dxa, dd_send, dd_recv, partner).wait_send()
+
+    for u in (units - 2, units - 1):
+        unit_sent(u).wait_send()
 
 
 def write_out(dxa, dxb, dwg, dwu, dwd, dx_ref, dwg_ref, dwu_ref, dwd_ref, sem):
@@ -336,8 +325,12 @@
             pltpu.VMEM((2 * UNIT, HALF), BF16),
             half, half,
             pltpu.VMEM((2, rows, UNIT), BF16),
-            dma((2,)), dma((4, 2)), dma((units,)), dma((2, 2)), dma((2,)),
-        ] + [dma((chunks,))] * 8,
+            dma((2,)), dma((2, 2)), dma((units,)), dma((2, 2)), dma((2,)),
+            dma((2,)), dma((chunks,)),
+            dma, dma((chunks,)),
+            dma, dma((chunks,)),
+            dma, dma,
+        ],
         compiler_params=pltpu.CompilerParams(
             collective_id=0, has_side_effects=True, vmem_limit_bytes=67043328 - 20 * 2**20),
         name="mlp_backward",

time: 128 us -> 125 us (0.977)
  Pallas kernels: 127 us -> 124 us
    pallas_call x1, Pallas kernels: 120 us -> 117 us  [backward(): pl.pallas_call(kernel, out_shape=[pltpu.VMEM((rows, HALF), BF16), pltpu.V...]
where the time goes in v4:
time: 125 us
  Pallas kernels  124 us (99%)
    pallas_call x1, Pallas kernels, backward(): pl.pallas_call(kernel, out_shape=[pltpu.VMEM((rows, HALF), BF16), pltpu.V...  117 us
    pallas_call x1, Pallas kernels, backward(): pl.pallas_call(write_out, out_shape=[jax.ShapeDtypeStruct((rows, d), BF16...  7.23 us

profile of v4, /device:TPU:0, one launch (start us, length us, event | category | flops | bytes accessed | tf_op | source)
XLA Modules:
  0.0 124.9 jit_solution(15071016770903174081)
XLA Ops:
  0.6 117.0 %mlp_backward.1 = (bf16[2048,1024]{1,0:T(8,128)(2,1)S(1)}, bf16[2048,1024]{1,0:T(8,128)(2,1)S(1)}, bf16[2048,1024]{1,0:T(8,128)(2,1)S(1)}, bf16[2048,1024]{1,0:T(8,128)(2,1)S(1)}, bf16[1024,2048]{1,0:T(8,128)(2,1)S(1)}) custom-call(bf16[2048,2048]{1,0:T(8,128)(2,1)} %x_ref.1, bf16[2048,2048]{1,0:T(8,128)(2,1)} %dy_ref.1, bf16[2048,1024]{1,0:T(8,128)(2,1)} %gate_ref.1, ...), custom_call_target="tpu_custom_call" | custom-call | tf_op jit(solution)/shard_map/mlp_backward/pallas_call | solution.py:312
  117.7 7.2 %write_out.1 = (bf16[2048,2048]{1,0:T(8,128)(2,1)}, bf16[2048,1024]{1,0:T(8,128)(2,1)}, bf16[2048,1024]{1,0:T(8,128)(2,1)}, bf16[1024,2048]{1,0:T(8,128)(2,1)}) custom-call(bf16[2048,1024]{1,0:T(8,128)(2,1)S(1)} %get-tuple-element.9.dxa, bf16[2048,1024]{1,0:T(8,128)(2,1)S(1)} %get-tuple-element.10.dxb, bf16[2048,1024]{1,0:T(8,128)(2,1)S(1)} %get-tuple-element.11.dwg, ...), custom_call_target="tpu_custom_call" | custom-call | tf_op jit(solution)/shard_map/write_out/pallas_call | solution.py:338
